TPU v7x, 128 devices: a whole 4x4x4 slice. The times are simulated.
128 devices in a mesh: data: 128 (over z, y, x, core).
Axes of the slice: x: 4, y: 4, z: 4, core: 2. Of those that a mesh axis runs over, the one named last changes fastest.
Arguments:
- act_in: bfloat16 [262144, 768], P('data')
- grad_out: bfloat16 [262144, 768], P('data')
- w_up: bfloat16 [2, 768, 2048], replicated
- w_down: bfloat16 [2, 2048, 768], replicated
- q_up: bfloat16 [2, 2048, 256], replicated
- q_down: bfloat16 [2, 768, 256], replicated
Outputs:
- output 1: bfloat16 [2, 768, 2048], replicated
- output 2: bfloat16 [2, 2048, 768], replicated
- output 3: float32 [2, 2048, 256], replicated
- output 4: float32 [2, 768, 256], replicated
All inputs are finite; a program needn't handle non-finite values.
Results may differ from a plain program's by a relative error of at most 0.0105384.
Values are sent between devices in bfloat16 or wider.
A program may use at most 1 GiB of HBM per device.

v0:
```python
import math
import functools
import jax
import jax.numpy as jnp
from jax import lax
from jax.experimental import pallas as pl
from jax.experimental.pallas import tpu as pltpu
from jax.sharding import PartitionSpec as P

MESH = pl.DeviceIdType.MESH
STRIDES = (2, 8, 32)
ORDERS = ((0, 1, 2), (1, 2, 0), (2, 0, 1))
COPIES = 47


def mat_nn(left_op, right_op):
    return jnp.dot(left_op, right_op, preferred_element_type=jnp.float32)


def mat_nt(left_op, right_op):
    return lax.dot_general(left_op, right_op, (((1,), (1,)), ((), ())), preferred_element_type=jnp.float32)


def mat_tn(left_op, right_op):
    return lax.dot_general(left_op, right_op, (((0,), (0,)), ((), ())), preferred_element_type=jnp.float32)


def flip(place, bit):
    if bit == 1:
        return place + 1 - 2 * lax.rem(place, 2)
    if bit == 2:
        return lax.rem(place + 2, 4)
    return 3 - place


def position(axis):
    me = lax.axis_index(axis)
    core = lax.rem(me, 2)
    places = tuple(lax.rem(lax.div(me, stride), 4) for stride in STRIDES)
    return me, core, places


def greet(pos):
    me, core, places = pos
    barrier = pltpu.get_barrier_semaphore()
    pl.semaphore_signal(barrier, inc=1, device_id=(me + 1 - 2 * core,), device_id_type=MESH)
    for dim in range(3):
        for bit in (1, 2, 3):
            peer = me + (flip(places[dim], bit) - places[dim]) * STRIDES[dim]
            pl.semaphore_signal(barrier, inc=1, device_id=(peer,), device_id_type=MESH)
    pl.semaphore_wait(barrier, 10)


class SumAll:
    def __init__(self, acc, bufs, sems, pos, lanes):
        self.acc, self.bufs, self.sems, self.pos = acc, bufs, sems, pos
        third = lanes // 3 // 128 * 128
        self.groups = ((0, third), (third, third), (2 * third, lanes - 2 * third))

    def rows(self, start, size, lo, width):
        return self.acc.at[pl.ds(pl.multiple_of(start, 8), size), pl.ds(lo, width)]

    def copies(self, phase):
        me, core, places = self.pos
        send, recv = self.sems[:2]
        lanes = self.acc.shape[1]
        out = []

        def add(index, src, dst, peer):
            out.append(pltpu.make_async_remote_copy(src_ref=src, dst_ref=dst, send_sem=send.at[index], recv_sem=recv.at[index], device_id=(peer,), device_id_type=MESH))

        partner = me + 1 - 2 * core
        if phase == 0:
            add(0, self.rows((1 - core) * 128, 128, 0, lanes), self.bufs[0], partner)
            return out
        if phase == 6:
            mine = self.rows(core * 128, 128, 0, lanes)
            add(46, mine, mine, partner)
            return out
        for group, (lo, width) in enumerate(self.groups):
            first, second, third = ORDERS[group]
            top = core * 128
            block = top + places[first] * 32
            base = block + places[second] * 8
            dim = {1: first, 2: second, 3: third, 4: second, 5: first}[phase]
            for bit in (1, 2, 3):
                other = flip(places[dim], bit)
                peer = me + (other - places[dim]) * STRIDES[dim]
                index = 1 + (phase - 1) * 9 + group * 3 + bit - 1
                if phase == 1:
                    src, dst = self.rows(top + other * 32, 32, lo, width), self.bufs[1].at[bit - 1, :, pl.ds(lo, width)]
                elif phase == 2:
                    src, dst = self.rows(block + other * 8, 8, lo, width), self.bufs[2].at[bit - 1, :, pl.ds(lo, width)]
                elif phase == 3:
                    src, dst = self.rows(base, 8, lo, width), self.bufs[3].at[bit - 1, :, pl.ds(lo, width)]
                elif phase == 4:
                    src = dst = self.rows(base, 8, lo, width)
                else:
                    src = dst = self.rows(block, 32, lo, width)
                add(index, src, dst, peer)
        return out

    def start(self, phase):
        if phase == 6:
            pl.semaphore_wait(self.sems[2], 1)
        for copy in self.copies(phase):
            copy.start()

    def finish(self, phase):
        for copy in self.copies(phase):
            copy.wait()
        me, core, places = self.pos
        if phase == 0:
            pl.semaphore_signal(self.sems[2], inc=1, device_id=(me + 1 - 2 * core,), device_id_type=MESH)
            mine = self.rows(core * 128, 128, 0, self.acc.shape[1])
            mine[...] += self.bufs[0][...]
            return
        if phase > 3:
            return
        for group, (lo, width) in enumerate(self.groups):
            first, second, third = ORDERS[group]
            block = core * 128 + places[first] * 32
            got = [self.bufs[phase][bit, :, pl.ds(lo, width)] for bit in range(3)]
            mine = self.rows(block, 32, lo, width) if phase == 1 else self.rows(block + places[second] * 8, 8, lo, width)
            mine[...] = (mine[...] + got[0]) + (got[1] + got[2])

    def step(self, phase):
        if phase > 0:
            self.finish(phase - 1)
        if phase < 7:
            self.start(phase)


TILE = 256
LANES = 256
ROOT = math.sqrt(2.0 / math.pi)


def gelu(z):
    half = 0.5 * z
    return half + half * jnp.tanh(z * (ROOT + (ROOT * 0.044715) * (z * z)))


def gelu_slope(z):
    square = z * z
    t = jnp.tanh(z * (ROOT + (ROOT * 0.044715) * square))
    return (0.5 + 0.5 * t) + (0.5 * z) * (1.0 - t * t) * (ROOT + (3.0 * ROOT * 0.044715) * square)


def tile_rows(i):
    return pl.ds(pl.multiple_of(i * TILE, TILE), TILE)


def step_kernel(axis, *refs):
    (x_hbm, dy_hbm, wu_hbm, wd_hbm, qu_hbm, qd_hbm, hat_u_hbm, hat_d_hbm, sum_u_hbm, sum_d_hbm,
     a0, z0, a1, z1, h1, g1, wu, wd, qu, qd, trans, stream_buf, pd1, pu1, pd0, pu0, extra,
     stream_sem, load_sem, out_sem, *rest) = refs
    tiles = x_hbm.shape[0] // TILE
    bf16 = jnp.bfloat16
    f32 = jnp.float32
    channels = [rest[7 * k:7 * k + 7] for k in range(5)]

    def load(index, src, dst):
        return pltpu.make_async_copy(src, dst, load_sem.at[index])

    def tile_copy(src, i, slot):
        return pltpu.make_async_copy(src.at[tile_rows(i)], stream_buf.at[slot], stream_sem.at[slot])

    def loop(body, hooks=None):
        def run(i, carry):
            for when, hook in (hooks or {}).items():
                pl.when(i == when)(hook)
            body(i)
            return carry
        lax.fori_loop(0, tiles, run, 0)

    def streamed(src, following, body, hooks=None):
        def run(i):
            slot = lax.rem(i, 2)

            @pl.when(i + 1 < tiles)
            def _():
                tile_copy(src, i + 1, 1 - slot).start()
            tile_copy(src, i, slot).wait()
            body(i, stream_buf.at[slot])
        loop(run, hooks)
        if following is not None:
            tile_copy(following, 0, 0).start()

    tile_copy(x_hbm, 0, 0).start()
    load_wu0 = load(0, wu_hbm.at[0], wu)
    load_wd0 = load(1, wd_hbm.at[0], wd)
    load_qd1 = load(2, qd_hbm.at[1], qd)
    load_qu1 = load(3, qu_hbm.at[1], qu)
    load_wu1 = load(4, wu_hbm.at[1], wu)
    load_wd1 = load(5, wd_hbm.at[1], wd)
    load_wd0b = load(6, wd_hbm.at[0], wd)
    load_qd0 = load(7, qd_hbm.at[0], qd)
    load_qu0 = load(8, qu_hbm.at[0], qu)
    load_wu0.start()
    load_wd0.start()
    load_qd1.start()
    load_qu1.start()
    pos = position(axis)
    greet(pos)

    def reducer(acc, channel):
        return SumAll(acc, channels[channel][:4], channels[channel][4:], pos, acc.shape[1])

    d1, u1, d0, u0 = reducer(pd1, 0), reducer(pu1, 2), reducer(pd0, 1), reducer(pu0, 3)
    q_d1, q_u1, q_d0, q_u0 = reducer(pu1, 2), reducer(pd1, 0), reducer(extra, 4), reducer(pd0, 1)

    def up_rows(i, left, pre, post):
        for n in range(0, pre.shape[1], LANES):
            z = mat_nn(left, wu[:, n:n + LANES]).astype(bf16)
            pre[tile_rows(i), n:n + LANES] = z
            post[tile_rows(i), n:n + LANES] = gelu(z.astype(f32)).astype(bf16)

    def cot_rows(i, cot, pre):
        for n in range(0, pre.shape[1], LANES):
            c = mat_nt(cot, wd[n:n + LANES, :])
            z = pre[tile_rows(i), n:n + LANES].astype(f32)
            pre[tile_rows(i), n:n + LANES] = (gelu_slope(z) * c).astype(bf16)

    def put_trans(i, value):
        trans[:, tile_rows(i)] = value.T.astype(bf16)

    def full_product(acc, right):
        for n in range(0, acc.shape[1], 256):
            acc[:, n:n + 256] = mat_nn(trans[...], right[:, n:n + 256])

    def normalise(acc, out, row, index, dst):
        def run(k, carry):
            rows = pl.ds(pl.multiple_of(k * 32, 32), 32)
            p = acc[rows, :]
            out[pl.ds(pl.multiple_of(row + k * 32, 32), 32), :] = (p / jnp.sqrt(jnp.sum(p * p, axis=1, keepdims=True))).astype(bf16)
            return carry
        lax.fori_loop(0, 8, run, 0)
        pltpu.make_async_copy(out.at[row:row + 256], dst, out_sem.at[index]).start()

    def z0_stage(i, x_tile):
        up_rows(i, x_tile[...], z0, a0)

    load_wu0.wait()
    streamed(x_hbm, x_hbm, z0_stage)
    load_wu1.start()
    load_wd0.wait()

    def h1_stage(i, x_tile):
        for n in range(0, h1.shape[1], 256):
            h1[tile_rows(i), n:n + 256] = (x_tile[:, n:n + 256].astype(f32) + mat_nn(a0[tile_rows(i), :], wd[:, n:n + 256])).astype(bf16)
    streamed(x_hbm, dy_hbm, h1_stage)
    load_wd1.start()
    load_wu1.wait()
    loop(lambda i: up_rows(i, h1[tile_rows(i), :], z1, a1))
    load_qd1.wait()

    def sd1_stage(i, dy_tile):
        put_trans(i, mat_nn(dy_tile[...], qd[...]))
    streamed(dy_hbm, dy_hbm, sd1_stage)
    load_qd0.start()
    full_product(pd1, a1)
    d1.step(0)
    load_wd1.wait()
    load_qu1.wait()

    def e1_stage(i, dy_tile):
        cot_rows(i, dy_tile[...], z1)
        put_trans(i, mat_nn(z1[tile_rows(i), :], qu[...]))
    streamed(dy_hbm, dy_hbm, e1_stage, {1: lambda: d1.step(1), 3: lambda: d1.step(2)})
    load_wd0b.start()
    load_qu0.start()
    full_product(pu1, h1)
    u1.step(0)

    def g1_stage(i, dy_tile):
        for n in range(0, g1.shape[1], 256):
            g1[tile_rows(i), n:n + 256] = (dy_tile[:, n:n + 256].astype(f32) + mat_nt(z1[tile_rows(i), :], wu[n:n + 256, :])).astype(bf16)

    def g1_second():
        u1.step(1)
        d1.step(4)

    def g1_fourth():
        d1.step(5)
        u1.step(3)
    streamed(dy_hbm, x_hbm, g1_stage, {0: lambda: d1.step(3), 1: g1_second, 2: lambda: u1.step(2), 3: g1_fourth})
    load_qd0.wait()
    loop(lambda i: put_trans(i, mat_nn(g1[tile_rows(i), :], qd[...])), {2: lambda: u1.step(4)})
    full_product(pd0, a0)
    d0.step(0)
    d1.step(6)
    u1.step(5)
    load_wd0b.wait()
    load_qu0.wait()

    def e0_stage(i, x_tile):
        cot_rows(i, g1[tile_rows(i), :], z0)
        sketch = mat_nn(z0[tile_rows(i), :], qu[...]).T.astype(bf16)
        part = mat_nn(sketch, x_tile[...])

        @pl.when(i == 0)
        def _():
            pu0[...] = part

        @pl.when(i > 0)
        def _():
            pu0[...] += part

    def e0_second():
        d0.step(1)
        d1.step(7)
        u1.step(6)

    def e0_third():
        u1.step(7)
        normalise(pd1, wu, 0, 0, hat_d_hbm.at[1])
    streamed(x_hbm, dy_hbm, e0_stage, {1: e0_second, 2: e0_third, 3: lambda: d0.step(2)})
    u0.step(0)
    d0.step(3)
    normalise(pu1, wd, 0, 1, hat_u_hbm.at[1])

    def qd1_stage(i, dy_tile):
        back = mat_nt(a1[tile_rows(i), :], wu[0:256, :]).T.astype(bf16)
        part = mat_nn(back, dy_tile[...])

        @pl.when(i == 0)
        def _():
            pu1[...] = part

        @pl.when(i > 0)
        def _():
            pu1[...] += part
    streamed(dy_hbm, x_hbm, qd1_stage, {2: lambda: (u0.step(1), d0.step(4)) and None})
    q_d1.step(0)
    u0.step(2)
    loop(lambda i: put_trans(i, mat_nt(h1[tile_rows(i), :], wd[0:256, :])))
    d0.step(5)
    full_product(pd1, z1)
    q_u1.step(0)
    u0.step(3)
    q_d1.step(1)
    d0.step(6)
    u0.step(4)
    q_u1.step(1)
    d0.step(7)
    normalise(pd0, wu, 256, 2, hat_d_hbm.at[0])
    u0.step(5)
    q_d1.step(2)
    loop(lambda i: put_trans(i, mat_nt(a0[tile_rows(i), :], wu[256:512, :])), {2: lambda: (u0.step(6), q_u1.step(2)) and None})
    full_product(extra, g1)
    q_d0.step(0)
    q_d1.step(3)
    u0.step(7)
    normalise(pu0, wd, 256, 3, hat_u_hbm.at[0])
    q_u1.step(3)

    def uu0_stage(i, x_tile):
        put_trans(i, mat_nt(x_tile[...], wd[256:512, :]))
    streamed(x_hbm, None, uu0_stage)
    q_d1.step(4)
    q_d0.step(1)
    full_product(pd0, z0)
    q_u0.step(0)
    q_u1.step(4)
    q_d1.step(5)
    q_d0.step(2)
    q_u0.step(1)
    q_u1.step(5)
    q_d1.step(6)
    q_d0.step(3)
    q_u0.step(2)
    q_d1.step(7)
    q_u1.step(6)
    q_d0.step(4)
    q_u0.step(3)
    q_u1.step(7)
    q_d0.step(5)
    q_u0.step(4)
    q_d0.step(6)
    q_u0.step(5)
    q_d0.step(7)
    q_u0.step(6)
    q_u0.step(7)
    results = [(pu1, sum_d_hbm.at[1]), (pd1, sum_u_hbm.at[1]), (extra, sum_d_hbm.at[0]), (pd0, sum_u_hbm.at[0])]
    outs = [pltpu.make_async_copy(src, dst, out_sem.at[4 + k]) for k, (src, dst) in enumerate(results)]
    for copy in outs:
        copy.start()
    hats = [(wu, 0, hat_d_hbm.at[1]), (wd, 0, hat_u_hbm.at[1]), (wu, 256, hat_d_hbm.at[0]), (wd, 256, hat_u_hbm.at[0])]
    for k, (src, row, dst) in enumerate(hats):
        pltpu.make_async_copy(src.at[row:row + 256], dst, out_sem.at[k]).wait()
    for copy in outs:
        copy.wait()


def sum_scratch(lanes):
    return [pltpu.VMEM((128, lanes), jnp.float32), pltpu.VMEM((3, 32, lanes), jnp.float32), pltpu.VMEM((3, 8, lanes), jnp.float32), pltpu.VMEM((3, 8, lanes), jnp.float32), pltpu.SemaphoreType.DMA((COPIES,)), pltpu.SemaphoreType.DMA((COPIES,)), pltpu.SemaphoreType.REGULAR]


def power_sums(axis, tok_rows, grad_rows, w_up, w_down, q_up, q_down):
    tokens, model = tok_rows.shape
    layers, _, wide = w_up.shape
    rank = q_up.shape[-1]
    bf16, f32 = jnp.bfloat16, jnp.float32
    scratch = [pltpu.VMEM((tokens, wide), bf16)] * 4 + [pltpu.VMEM((tokens, model), bf16)] * 2
    scratch += [pltpu.VMEM((model, wide), bf16), pltpu.VMEM((wide, model), bf16), pltpu.VMEM((wide, rank), bf16), pltpu.VMEM((model, rank), bf16)]
    scratch += [pltpu.VMEM((rank, tokens), bf16), pltpu.VMEM((2, TILE, model), bf16)]
    scratch += [pltpu.VMEM((rank, lanes), f32) for lanes in (wide, model, wide, model, model)]
    scratch += [pltpu.SemaphoreType.DMA((2,)), pltpu.SemaphoreType.DMA((9,)), pltpu.SemaphoreType.DMA((8,))]
    for lanes in (wide, wide, model, model, model):
        scratch += sum_scratch(lanes)
    return pl.pallas_call(
        functools.partial(step_kernel, axis),
        out_shape=[jax.ShapeDtypeStruct((layers, rank, model), bf16), jax.ShapeDtypeStruct((layers, rank, wide), bf16), jax.ShapeDtypeStruct((layers, rank, wide), f32), jax.ShapeDtypeStruct((layers, rank, model), f32)],
        in_specs=[pl.BlockSpec(memory_space=pl.ANY)] * 6,
        out_specs=[pl.BlockSpec(memory_space=pl.ANY)] * 4,
        scratch_shapes=scratch,
        compiler_params=pltpu.CompilerParams(collective_id=0, has_side_effects=True, vmem_limit_bytes=67043328),
        name="power_sums",
    )(tok_rows, grad_rows, w_up, w_down, q_up, q_down)


def update_kernel(step_size, hat_u, hat_d, sum_u, sum_d, sum_u_part, sum_d_part, w_up, w_down, up_new, down_new, up_fac, down_fac):
    up_new[0] = (w_up[0].astype(jnp.float32) - step_size * mat_tn(hat_u[0], sum_u[0].astype(jnp.bfloat16))).astype(jnp.bfloat16)
    down_new[0] = (w_down[0].astype(jnp.float32) - step_size * mat_tn(hat_d[0], sum_d[0].astype(jnp.bfloat16))).astype(jnp.bfloat16)
    up_fac[0] = sum_u_part[0].T
    down_fac[0] = sum_d_part[0].T


def update(step_size, hat_u, hat_d, sum_u, sum_d, w_up, w_down):
    layers, model, wide = w_up.shape
    rank = hat_u.shape[1]
    parts = 2
    bf16, f32 = jnp.bfloat16, jnp.float32

    def cols(lanes):
        return pl.BlockSpec((1, rank, lanes // parts), lambda l, p: (l, 0, p))

    def whole(lanes):
        return pl.BlockSpec((1, rank, lanes), lambda l, p: (l, 0, 0))

    def rows(count, lanes):
        return pl.BlockSpec((1, count // parts, lanes), lambda l, p: (l, p, 0))

    return pl.pallas_call(
        functools.partial(update_kernel, step_size),
        grid=(layers, parts),
        in_specs=[cols(model), cols(wide), whole(wide), whole(model), cols(wide), cols(model), rows(model, wide), rows(wide, model)],
        out_specs=[rows(model, wide), rows(wide, model), rows(wide, rank), rows(model, rank)],
        out_shape=[jax.ShapeDtypeStruct((layers, model, wide), bf16), jax.ShapeDtypeStruct((layers, wide, model), bf16), jax.ShapeDtypeStruct((layers, wide, rank), f32), jax.ShapeDtypeStruct((layers, model, rank), f32)],
        compiler_params=pltpu.CompilerParams(vmem_limit_bytes=56 * 2**20),
        name="update",
    )(hat_u, hat_d, sum_u, sum_d, sum_u, sum_d, w_up, w_down)


def solution(mesh):
    axis = mesh.axis_names[0]

    def local_step(tok_rows, grad_rows, w_up, w_down, q_up, q_down):
        step_size = 0.4 / math.sqrt(q_up.shape[-1])
        hat_u, hat_d, sum_u, sum_d = power_sums(axis, tok_rows, grad_rows, w_up, w_down, q_up, q_down)
        return tuple(update(step_size, hat_u, hat_d, sum_u, sum_d, w_up, w_down))

    row_spec = P(axis, None)
    return jax.shard_map(local_step, mesh=mesh, in_specs=(row_spec, row_spec, P(), P(), P(), P()), out_specs=(P(), P(), P(), P()), check_vma=False)
```

profile of v0, /device:TPU:1, one launch (start us, length us, event | category | flops | bytes accessed | tf_op | source)
XLA Modules:
  0.0 206.2 jit_solution(14343210116122638105)
XLA Ops:
  0.6 190.0 %power_sums.1 = (bf16[2,256,768]{2,1,0:T(8,128)(2,1)}, bf16[2,256,2048]{2,1,0:T(8,128)(2,1)}, f32[2,256,2048]{2,1,0:T(8,128)}, f32[2,256,768]{2,1,0:T(8,128)}) custom-call(bf16[2048,768]{1,0:T(8,128)(2,1)} %refs_0_.1, bf16[2048,768]{1,0:T(8,128)(2,1)} %refs_1_.1, bf16[2,768,2048]{2,1,0:T(8,128)(2,1)} %w_up.1, bf16[2,2048,768]{2,1,0:T(8,128)(2,1)} %w_down.1, ...), custom_call_target="tpu_custom_call" | custom-call | tf_op jit(solution)/shard_map/power_sums/pallas_call | solution.py:412
  190.6 15.4 %update.1 = (bf16[2,768,2048]{2,1,0:T(8,128)(2,1)}, bf16[2,2048,768]{2,1,0:T(8,128)(2,1)}, f32[2,2048,256]{2,1,0:T(8,128)}, f32[2,768,256]{2,1,0:T(8,128)}) custom-call(bf16[2,256,768]{2,1,0:T(8,128)(2,1)} %get-tuple-element.8.hat_u, bf16[2,256,2048]{2,1,0:T(8,128)(2,1)} %get-tuple-element.9.hat_d, f32[2,256,2048]{2,1,0:T(8,128)} %get-tuple-element.10.sum_u.sum_u_part, ...), custom_call_target="tpu_custom_call" | custom-call | tf_op jit(solution)/shard_map/update/pallas_call | solution.py:445
where the time goes:
time: 207 us; the launch traced here: 206 us
  Pallas kernels  205 us (99%)
    pallas_call x1, Pallas kernels, power_sums(): pl.pallas_call(functools.partial(step_kernel, axis), out_shape=[jax.Shape...  190 us
    pallas_call x1, Pallas kernels, update(): pl.pallas_call(functools.partial(update_kernel, step_size), grid=(layers,...  15.4 us

commit v1 on v0

--- a/solution.py
+++ b/solution.py
@@ -112,17 +112,21 @@
         me, core, places = self.pos
         if phase == 0:
             pl.semaphore_signal(self.sems[2], inc=1, device_id=(me + 1 - 2 * core,), device_id_type=MESH)
-            mine = self.rows(core * 128, 128, 0, self.acc.shape[1])
-            mine[...] += self.bufs[0][...]
+            def add(k, carry):
+                mine = self.rows(core * 128 + k * 8, 8, 0, self.acc.shape[1])
+                mine[...] += self.bufs[0][pl.ds(pl.multiple_of(k * 8, 8), 8), :]
+                return carry
+            lax.fori_loop(0, 16, add, 0)
             return
         if phase > 3:
             return
         for group, (lo, width) in enumerate(self.groups):
             first, second, third = ORDERS[group]
             block = core * 128 + places[first] * 32
-            got = [self.bufs[phase][bit, :, pl.ds(lo, width)] for bit in range(3)]
-            mine = self.rows(block, 32, lo, width) if phase == 1 else self.rows(block + places[second] * 8, 8, lo, width)
-            mine[...] = (mine[...] + got[0]) + (got[1] + got[2])
+            for k in range(4 if phase == 1 else 1):
+                got = [self.bufs[phase][bit, k * 8:k * 8 + 8, pl.ds(lo, width)] for bit in range(3)]
+                mine = self.rows(block + k * 8 if phase == 1 else block + places[second] * 8, 8, lo, width)
+                mine[...] = (mine[...] + got[0]) + (got[1] + got[2])
 
     def step(self, phase):
         if phase > 0:
@@ -131,7 +135,27 @@
             self.start(phase)
 
 
-TILE = 256
+PLAN = {'e1_1': ('d1',),
+ 'e1_3': ('d1',),
+ 'pu1': ('d1',),
+ 'g1_1': ('u1', 'd1'),
+ 'g1_3': ('u1', 'd1'),
+ 'sd0_0': ('u1',),
+ 'e0_0': ('d1', 'u1'),
+ 'e0_1': ('d0', 'u1', 'd1', 'hd1'),
+ 'e0_3': ('d0', 'u1'),
+ 'hats1': ('u1', 'd0'),
+ 'qd1_1': ('u0',),
+ 'qd1_2': ('d0',),
+ 'uu1_0': ('u0', 'd0'),
+ 'uu1_2': ('qd1',),
+ 'qu1': ('u0',),
+ 'hd0': ('d0', 'qu1', 'qd1', 'u0', 'd0'),
+ 'hu0': ('qu1', 'qd1', 'u0', 'qu1', 'qd1', 'u0', 'qu1', 'u0', 'qd1'),
+ 'uu0_2': ('qu1', 'qd0'),
+ 'uu0_3': ('qd1',),
+ 'end': ('qd1', 'qu1', 'qu0', 'qd0', 'qu1', 'qu0', 'qd0', 'qu0', 'qd0', 'qu0', 'qd0', 'qu0', 'qd0', 'qd0', 'qu0', 'qu0')}
+TILE = 512
 LANES = 256
 ROOT = math.sqrt(2.0 / math.pi)
 
@@ -153,12 +177,12 @@
 
 def step_kernel(axis, *refs):
     (x_hbm, dy_hbm, wu_hbm, wd_hbm, qu_hbm, qd_hbm, hat_u_hbm, hat_d_hbm, sum_u_hbm, sum_d_hbm,
-     a0, z0, a1, z1, h1, g1, wu, wd, qu, qd, trans, stream_buf, pd1, pu1, pd0, pu0, extra,
+     a0, z0, a1, z1, h1, g1, wu, wd, qu, qd, trans, stream_buf, pd1, pu1, pd0, pu0,
      stream_sem, load_sem, out_sem, *rest) = refs
     tiles = x_hbm.shape[0] // TILE
     bf16 = jnp.bfloat16
     f32 = jnp.float32
-    channels = [rest[7 * k:7 * k + 7] for k in range(5)]
+    channels = [rest[7 * k:7 * k + 7] for k in range(4)]
 
     def load(index, src, dst):
         return pltpu.make_async_copy(src, dst, load_sem.at[index])
@@ -207,8 +231,23 @@
     def reducer(acc, channel):
         return SumAll(acc, channels[channel][:4], channels[channel][4:], pos, acc.shape[1])
 
-    d1, u1, d0, u0 = reducer(pd1, 0), reducer(pu1, 2), reducer(pd0, 1), reducer(pu0, 3)
-    q_d1, q_u1, q_d0, q_u0 = reducer(pu1, 2), reducer(pd1, 0), reducer(extra, 4), reducer(pd0, 1)
+    places = {"d1": (pd1, 0), "u1": (pu1, 2), "d0": (pd0, 1), "u0": (pu0, 3), "qd1": (pu1, 2), "qu1": (pd1, 0), "qd0": (pu0, 3), "qu0": (pd0, 1)}
+    sums = {name: reducer(*place) for name, place in places.items()}
+    phases = dict.fromkeys(places, 0)
+
+    def act(key):
+        for name in PLAN.get(key, ()):
+            if name == "hd1":
+                normalise(pd1, wu, 0, 0, hat_d_hbm.at[1])
+            else:
+                advance(name)
+
+    def advance(name):
+        sums[name].step(phases[name])
+        phases[name] += 1
+
+    def hooks(stage):
+        return {i: functools.partial(act, stage + str(i)) for i in range(4) if PLAN.get(stage + str(i))}
 
     def up_rows(i, left, pre, post):
         for n in range(0, pre.shape[1], LANES):
@@ -228,6 +267,13 @@
     def full_product(acc, right):
         for n in range(0, acc.shape[1], 256):
             acc[:, n:n + 256] = mat_nn(trans[...], right[:, n:n + 256])
+
+    def add_product(i, acc, left, right):
+        @pl.when(i == 0)
+        def _():
+            acc[...] = jnp.zeros_like(acc)
+        for n in range(0, acc.shape[1], 256):
+            acc[:, n:n + 256] += mat_nn(left, right[:, n:n + 256])
 
     def normalise(acc, out, row, index, dst):
         def run(k, carry):
@@ -260,129 +306,67 @@
     streamed(dy_hbm, dy_hbm, sd1_stage)
     load_qd0.start()
     full_product(pd1, a1)
-    d1.step(0)
+    advance("d1")
     load_wd1.wait()
     load_qu1.wait()
 
     def e1_stage(i, dy_tile):
         cot_rows(i, dy_tile[...], z1)
         put_trans(i, mat_nn(z1[tile_rows(i), :], qu[...]))
-    streamed(dy_hbm, dy_hbm, e1_stage, {1: lambda: d1.step(1), 3: lambda: d1.step(2)})
+    streamed(dy_hbm, dy_hbm, e1_stage, hooks("e1_"))
     load_wd0b.start()
     load_qu0.start()
+    act("pu1")
     full_product(pu1, h1)
-    u1.step(0)
+    advance("u1")
 
     def g1_stage(i, dy_tile):
         for n in range(0, g1.shape[1], 256):
             g1[tile_rows(i), n:n + 256] = (dy_tile[:, n:n + 256].astype(f32) + mat_nt(z1[tile_rows(i), :], wu[n:n + 256, :])).astype(bf16)
-
-    def g1_second():
-        u1.step(1)
-        d1.step(4)
-
-    def g1_fourth():
-        d1.step(5)
-        u1.step(3)
-    streamed(dy_hbm, x_hbm, g1_stage, {0: lambda: d1.step(3), 1: g1_second, 2: lambda: u1.step(2), 3: g1_fourth})
+    streamed(dy_hbm, x_hbm, g1_stage, hooks("g1_"))
     load_qd0.wait()
-    loop(lambda i: put_trans(i, mat_nn(g1[tile_rows(i), :], qd[...])), {2: lambda: u1.step(4)})
+    loop(lambda i: put_trans(i, mat_nn(g1[tile_rows(i), :], qd[...])), hooks("sd0_"))
+    act("pd0")
     full_product(pd0, a0)
-    d0.step(0)
-    d1.step(6)
-    u1.step(5)
+    advance("d0")
     load_wd0b.wait()
     load_qu0.wait()
 
     def e0_stage(i, x_tile):
         cot_rows(i, g1[tile_rows(i), :], z0)
         sketch = mat_nn(z0[tile_rows(i), :], qu[...]).T.astype(bf16)
-        part = mat_nn(sketch, x_tile[...])
-
-        @pl.when(i == 0)
-        def _():
-            pu0[...] = part
-
-        @pl.when(i > 0)
-        def _():
-            pu0[...] += part
-
-    def e0_second():
-        d0.step(1)
-        d1.step(7)
-        u1.step(6)
-
-    def e0_third():
-        u1.step(7)
-        normalise(pd1, wu, 0, 0, hat_d_hbm.at[1])
-    streamed(x_hbm, dy_hbm, e0_stage, {1: e0_second, 2: e0_third, 3: lambda: d0.step(2)})
-    u0.step(0)
-    d0.step(3)
+        add_product(i, pu0, sketch, x_tile)
+    streamed(x_hbm, dy_hbm, e0_stage, hooks("e0_"))
+    advance("u0")
+    act("hats1")
     normalise(pu1, wd, 0, 1, hat_u_hbm.at[1])
 
     def qd1_stage(i, dy_tile):
         back = mat_nt(a1[tile_rows(i), :], wu[0:256, :]).T.astype(bf16)
-        part = mat_nn(back, dy_tile[...])
-
-        @pl.when(i == 0)
-        def _():
-            pu1[...] = part
-
-        @pl.when(i > 0)
-        def _():
-            pu1[...] += part
-    streamed(dy_hbm, x_hbm, qd1_stage, {2: lambda: (u0.step(1), d0.step(4)) and None})
-    q_d1.step(0)
-    u0.step(2)
-    loop(lambda i: put_trans(i, mat_nt(h1[tile_rows(i), :], wd[0:256, :])))
-    d0.step(5)
+        add_product(i, pu1, back, dy_tile)
+    streamed(dy_hbm, x_hbm, qd1_stage, hooks("qd1_"))
+    advance("qd1")
+    loop(lambda i: put_trans(i, mat_nt(h1[tile_rows(i), :], wd[0:256, :])), hooks("uu1_"))
+    act("qu1")
     full_product(pd1, z1)
-    q_u1.step(0)
-    u0.step(3)
-    q_d1.step(1)
-    d0.step(6)
-    u0.step(4)
-    q_u1.step(1)
-    d0.step(7)
+    advance("qu1")
+    act("hd0")
     normalise(pd0, wu, 256, 2, hat_d_hbm.at[0])
-    u0.step(5)
-    q_d1.step(2)
-    loop(lambda i: put_trans(i, mat_nt(a0[tile_rows(i), :], wu[256:512, :])), {2: lambda: (u0.step(6), q_u1.step(2)) and None})
-    full_product(extra, g1)
-    q_d0.step(0)
-    q_d1.step(3)
-    u0.step(7)
+    loop(lambda i: put_trans(i, mat_nt(a0[tile_rows(i), :], wu[256:512, :])), hooks("ud0_"))
+    act("hu0")
     normalise(pu0, wd, 256, 3, hat_u_hbm.at[0])
-    q_u1.step(3)
+    full_product(pu0, g1)
+    advance("qd0")
 
     def uu0_stage(i, x_tile):
         put_trans(i, mat_nt(x_tile[...], wd[256:512, :]))
-    streamed(x_hbm, None, uu0_stage)
-    q_d1.step(4)
-    q_d0.step(1)
+    streamed(x_hbm, None, uu0_stage, hooks("uu0_"))
+    act("qu0")
     full_product(pd0, z0)
-    q_u0.step(0)
-    q_u1.step(4)
-    q_d1.step(5)
-    q_d0.step(2)
-    q_u0.step(1)
-    q_u1.step(5)
-    q_d1.step(6)
-    q_d0.step(3)
-    q_u0.step(2)
-    q_d1.step(7)
-    q_u1.step(6)
-    q_d0.step(4)
-    q_u0.step(3)
-    q_u1.step(7)
-    q_d0.step(5)
-    q_u0.step(4)
-    q_d0.step(6)
-    q_u0.step(5)
-    q_d0.step(7)
-    q_u0.step(6)
-    q_u0.step(7)
-    results = [(pu1, sum_d_hbm.at[1]), (pd1, sum_u_hbm.at[1]), (extra, sum_d_hbm.at[0]), (pd0, sum_u_hbm.at[0])]
+    advance("qu0")
+    act("end")
+    assert set(phases.values()) == {8}
+    results = [(pu1, sum_d_hbm.at[1]), (pd1, sum_u_hbm.at[1]), (pu0, sum_d_hbm.at[0]), (pd0, sum_u_hbm.at[0])]
     outs = [pltpu.make_async_copy(src, dst, out_sem.at[4 + k]) for k, (src, dst) in enumerate(results)]
     for copy in outs:
         copy.start()
@@ -405,9 +389,9 @@
     scratch = [pltpu.VMEM((tokens, wide), bf16)] * 4 + [pltpu.VMEM((tokens, model), bf16)] * 2
     scratch += [pltpu.VMEM((model, wide), bf16), pltpu.VMEM((wide, model), bf16), pltpu.VMEM((wide, rank), bf16), pltpu.VMEM((model, rank), bf16)]
     scratch += [pltpu.VMEM((rank, tokens), bf16), pltpu.VMEM((2, TILE, model), bf16)]
-    scratch += [pltpu.VMEM((rank, lanes), f32) for lanes in (wide, model, wide, model, model)]
+    scratch += [pltpu.VMEM((rank, lanes), f32) for lanes in (wide, model, wide, model)]
     scratch += [pltpu.SemaphoreType.DMA((2,)), pltpu.SemaphoreType.DMA((9,)), pltpu.SemaphoreType.DMA((8,))]
-    for lanes in (wide, wide, model, model, model):
+    for lanes in (wide, wide, model, model):
         scratch += sum_scratch(lanes)
     return pl.pallas_call(
         functools.partial(step_kernel, axis),
@@ -420,37 +404,41 @@
     )(tok_rows, grad_rows, w_up, w_down, q_up, q_down)
 
 
-def update_kernel(step_size, hat_u, hat_d, sum_u, sum_d, sum_u_part, sum_d_part, w_up, w_down, up_new, down_new, up_fac, down_fac):
+def update_kernel(step_size, hat_u, hat_d, sum_u, sum_d, w_up, w_down, up_new, down_new, up_fac, down_fac):
     up_new[0] = (w_up[0].astype(jnp.float32) - step_size * mat_tn(hat_u[0], sum_u[0].astype(jnp.bfloat16))).astype(jnp.bfloat16)
     down_new[0] = (w_down[0].astype(jnp.float32) - step_size * mat_tn(hat_d[0], sum_d[0].astype(jnp.bfloat16))).astype(jnp.bfloat16)
-    up_fac[0] = sum_u_part[0].T
-    down_fac[0] = sum_d_part[0].T
+    up_fac[0] = sum_u[0].T
+
+    @pl.when(pl.program_id(1) == 0)
+    def _():
+        down_fac[0] = sum_d[0].T
 
 
 def update(step_size, hat_u, hat_d, sum_u, sum_d, w_up, w_down):
     layers, model, wide = w_up.shape
     rank = hat_u.shape[1]
-    parts = 2
+    parts = 4
+    part = wide // parts
     bf16, f32 = jnp.bfloat16, jnp.float32
 
-    def cols(lanes):
-        return pl.BlockSpec((1, rank, lanes // parts), lambda l, p: (l, 0, p))
-
-    def whole(lanes):
-        return pl.BlockSpec((1, rank, lanes), lambda l, p: (l, 0, 0))
-
-    def rows(count, lanes):
-        return pl.BlockSpec((1, count // parts, lanes), lambda l, p: (l, p, 0))
+    def cols(count):
+        return pl.BlockSpec((1, count, part), lambda l, p: (l, 0, p))
+
+    def rows(lanes):
+        return pl.BlockSpec((1, part, lanes), lambda l, p: (l, p, 0))
+
+    def whole(count, lanes):
+        return pl.BlockSpec((1, count, lanes), lambda l, p: (l, 0, 0))
 
     return pl.pallas_call(
         functools.partial(update_kernel, step_size),
         grid=(layers, parts),
-        in_specs=[cols(model), cols(wide), whole(wide), whole(model), cols(wide), cols(model), rows(model, wide), rows(wide, model)],
-        out_specs=[rows(model, wide), rows(wide, model), rows(wide, rank), rows(model, rank)],
+        in_specs=[whole(rank, model), cols(rank), cols(rank), whole(rank, model), cols(model), rows(model)],
+        out_specs=[cols(model), rows(model), rows(rank), whole(model, rank)],
         out_shape=[jax.ShapeDtypeStruct((layers, model, wide), bf16), jax.ShapeDtypeStruct((layers, wide, model), bf16), jax.ShapeDtypeStruct((layers, wide, rank), f32), jax.ShapeDtypeStruct((layers, model, rank), f32)],
         compiler_params=pltpu.CompilerParams(vmem_limit_bytes=56 * 2**20),
         name="update",
-    )(hat_u, hat_d, sum_u, sum_d, sum_u, sum_d, w_up, w_down)
+    )(hat_u, hat_d, sum_u, sum_d, w_up, w_down)
 
 
 def solution(mesh):

time: 207 us -> 188 us (0.908)
  Pallas kernels: 205 us -> 187 us
    pallas_call x1, Pallas kernels: 190 us -> 170 us  [power_sums(): pl.pallas_call(functools.partial(step_kernel, axis), out_shape=[jax.Shape...]
where the time goes in v1:
time: 188 us
  Pallas kernels  187 us (99%)
    pallas_call x1, Pallas kernels, power_sums(): pl.pallas_call(functools.partial(step_kernel, axis), out_shape=[jax.Shape...  170 us
    pallas_call x1, Pallas kernels, update(): pl.pallas_call(functools.partial(update_kernel, step_size), grid=(layers,...  17.4 us

profile of v1, /device:TPU:1, one launch (start us, length us, event | category | flops | bytes accessed | tf_op | source)
XLA Modules:
  0.0 188.0 jit_solution(6261304491615977424)
XLA Ops:
  0.6 169.9 %power_sums.1 = (bf16[2,256,768]{2,1,0:T(8,128)(2,1)}, bf16[2,256,2048]{2,1,0:T(8,128)(2,1)}, f32[2,256,2048]{2,1,0:T(8,128)}, f32[2,256,768]{2,1,0:T(8,128)}) custom-call(bf16[2048,768]{1,0:T(8,128)(2,1)} %refs_0_.1, bf16[2048,768]{1,0:T(8,128)(2,1)} %refs_1_.1, bf16[2,768,2048]{2,1,0:T(8,128)(2,1)} %w_up.1, bf16[2,2048,768]{2,1,0:T(8,128)(2,1)} %w_down.1, ...), custom_call_target="tpu_custom_call" | custom-call | tf_op jit(solution)/shard_map/power_sums/pallas_call | solution.py:396
  170.6 17.4 %update.1 = (bf16[2,768,2048]{2,1,0:T(8,128)(2,1)}, bf16[2,2048,768]{2,1,0:T(8,128)(2,1)}, f32[2,2048,256]{2,1,0:T(8,128)}, f32[2,768,256]{2,1,0:T(8,128)}) custom-call(bf16[2,256,768]{2,1,0:T(8,128)(2,1)} %get-tuple-element.8.hat_u, bf16[2,256,2048]{2,1,0:T(8,128)(2,1)} %get-tuple-element.9.hat_d, f32[2,256,2048]{2,1,0:T(8,128)} %get-tuple-element.10.sum_u, ...), custom_call_target="tpu_custom_call" | custom-call | tf_op jit(solution)/shard_map/update/pallas_call | solution.py:433
